TPU v7x, 32 devices: a whole 2x2x4 slice. The times are simulated.
32 devices in a mesh: clip: 4 (over y, core), seq: 8 (over z, x).
Axes of the slice: x: 2, y: 2, z: 4, core: 2. Of those that a mesh axis runs over, the one named last changes fastest.
Arguments:
- block_input: bfloat16 [64, 384, 1152], P('clip', 'seq'), parts along dimension 0, may hold values from -160 to 160
- mid_state: bfloat16 [64, 384, 1152], P('clip', 'seq'), parts along dimension 0, may hold values from -160 to 160
- saved_qkv: bfloat16 [3, 64, 384, 576], P(None, 'clip', 'seq'), parts along dimension 1, may hold values from -6 to 6
- out_grad: bfloat16 [64, 384, 1152], P('clip', 'seq'), parts along dimension 0, may hold values from -6 to 6
- modulation: float32 [20, 1152], P('clip'), parts along dimension 0, may hold values from -3 to 3
- w_qkv_s: bfloat16 [1152, 1728], replicated, may hold values from -0.1875 to 0.1875
- w_out_s: bfloat16 [576, 1152], replicated, may hold values from -0.25 to 0.25
- w_qkv_t: bfloat16 [1152, 1728], replicated, may hold values from -0.1875 to 0.1875
- w_out_t: bfloat16 [576, 1152], replicated, may hold values from -0.25 to 0.25
- qk_gain: float32 [4, 72], replicated, may hold values from 0.1 to 1.9
Outputs:
- input_grad: bfloat16 [64, 384, 1152], P('clip', 'seq'), parts along dimension 0
- mod_grad: float32 [24, 1152], P('clip'), parts along dimension 0
There are 4 independent parts, one for each index of `clip`. A program takes and returns all parts, laid end to end along the dimension named above; an argument that names none is the same for every part. Nothing has to cross between parts.
All inputs are finite; a program needn't handle non-finite values.
Results may differ from a plain program's by a relative error of at most 0.0057.
Values may be sent and summed in bfloat16 or wider, within the bound.
No kernel may reach another device: no remote copies, remote signals or barrier semaphores. Data moves between devices by JAX's collectives and lax.ppermute only.
A program may use at most 128 MiB of HBM per device.

v0:
```python
import jax
import jax.numpy as jnp
from jax import lax
from jax.sharding import PartitionSpec as P

HEADS = 8
HEAD_DIM = 72
WIDTH = 576


NORM_EPS = 1e-06


def layer_stats(inputs):
    values = inputs.astype(jnp.float32)
    centre = jnp.mean(values, axis=-1, keepdims=True)
    spread = jnp.mean(jnp.square(values - centre), axis=-1, keepdims=True)
    inverse = lax.rsqrt(spread + NORM_EPS)
    return ((values - centre) * inverse, inverse)


def modulate(normed, offset, stretch):
    return (normed * (1.0 + stretch) + offset).astype(jnp.bfloat16)


def matmul_rows(left_rows, weight):
    flattened = left_rows.reshape(-1, left_rows.shape[-1])
    result = jnp.dot(flattened, weight, preferred_element_type=jnp.float32)
    return result.reshape(left_rows.shape[:-1] + (weight.shape[1],))


def matmul_back(left_rows, weight):
    flattened = left_rows.reshape(-1, left_rows.shape[-1])
    result = lax.dot_general(
        flattened, weight, (((1,), (1,)), ((), ())), preferred_element_type=jnp.float32
    )
    return result.reshape(left_rows.shape[:-1] + (weight.shape[0],))


def head_split(tensor):
    return tensor.reshape(tensor.shape[:-1] + (HEADS, HEAD_DIM))


def rms_normed(raw_rows, gain_row):
    values = head_split(raw_rows).astype(jnp.float32)
    inverse = lax.rsqrt(jnp.mean(values * values, axis=-1, keepdims=True) + NORM_EPS)
    return ((values * inverse * gain_row).astype(jnp.bfloat16), values, inverse)


def rms_back(values, inverse, gain_row, upstream):
    scaled = gain_row * upstream
    result = inverse * scaled - values * (inverse * inverse * inverse) * jnp.mean(
        values * scaled, axis=-1, keepdims=True
    )
    return result.astype(jnp.bfloat16).reshape(values.shape[:-2] + (-1,))


def attend(queries, key_rows, value_rows, out_cot, query_gain, key_gain):
    query_norm, query_raw, query_inv = rms_normed(queries, query_gain)
    key_norm, key_raw, key_inv = rms_normed(key_rows, key_gain)
    factor = HEAD_DIM ** (-0.5)
    scores = (
        jnp.einsum("blhd,bmhd->bhlm", query_norm, key_norm, preferred_element_type=jnp.float32)
        * factor
    )
    exp_scores = jnp.exp(scores)
    attn_probs = exp_scores / jnp.sum(exp_scores, axis=-1, keepdims=True)
    probs_half = attn_probs.astype(jnp.bfloat16)
    value_heads = head_split(value_rows)
    cot_heads = head_split(out_cot)
    outputs = jnp.einsum(
        "bhlm,bmhd->blhd", probs_half, value_heads, preferred_element_type=jnp.float32
    ).astype(jnp.bfloat16)
    prob_grad = jnp.einsum(
        "blhd,bmhd->bhlm", cot_heads, value_heads, preferred_element_type=jnp.float32
    )
    row_inner = jnp.sum(attn_probs * prob_grad, axis=-1, keepdims=True)
    score_grad = (attn_probs * (prob_grad - row_inner) * factor).astype(jnp.bfloat16)
    value_grad = jnp.einsum(
        "bhlm,blhd->bmhd", probs_half, cot_heads, preferred_element_type=jnp.float32
    ).astype(jnp.bfloat16)
    qnorm_grad = jnp.einsum(
        "bhlm,bmhd->blhd", score_grad, key_norm, preferred_element_type=jnp.float32
    )
    knorm_grad = jnp.einsum(
        "bhlm,blhd->bmhd", score_grad, query_norm, preferred_element_type=jnp.float32
    )
    merged = outputs.shape[:-2] + (-1,)
    return (
        outputs.reshape(merged),
        rms_back(query_raw, query_inv, query_gain, qnorm_grad),
        rms_back(key_raw, key_inv, key_gain, knorm_grad),
        value_grad.reshape(merged),
    )


def output_cot(cotangent, gate_row, w_out):
    scaled = (cotangent.astype(jnp.float32) * gate_row).astype(jnp.bfloat16)
    return matmul_back(scaled, w_out).astype(jnp.bfloat16)


def gate_term(cotangent, outputs, w_out):
    branch = matmul_rows(outputs, w_out)
    return jnp.sum((cotangent.astype(jnp.float32) * branch).reshape(-1, branch.shape[-1]), axis=0)


def input_branch(grad_parts, w_qkv, normed, inverse, stretch):
    joined = jnp.concatenate(grad_parts, axis=-1)
    mod_cot = matmul_back(joined, w_qkv)
    columns = mod_cot.shape[-1]
    offset_term = jnp.sum(mod_cot.reshape(-1, columns), axis=0)
    stretch_term = jnp.sum((mod_cot * normed).reshape(-1, columns), axis=0)
    norm_cot = mod_cot * (1.0 + stretch)
    branch = inverse * (
        norm_cot
        - jnp.mean(norm_cot, axis=-1, keepdims=True)
        - normed * jnp.mean(norm_cot * normed, axis=-1, keepdims=True)
    )
    return (branch, offset_term, stretch_term)


def swapped(tensor):
    return jnp.swapaxes(tensor, 0, 1)


def body(
    block_input,
    mid_state,
    saved_qkv,
    out_grad,
    modulation,
    w_qkv_s,
    w_out_s,
    w_qkv_t,
    w_out_t,
    qk_gain,
):
    normed_mid, inverse_mid = layer_stats(mid_state)
    temporal_cot = output_cot(out_grad, modulation[4], w_out_t)
    temporal_res = attend(
        swapped(saved_qkv[0]),
        swapped(saved_qkv[1]),
        swapped(saved_qkv[2]),
        swapped(temporal_cot),
        qk_gain[2],
        qk_gain[3],
    )
    temporal_gate = gate_term(out_grad, swapped(temporal_res[0]), w_out_t)
    temporal_branch, temporal_offset, temporal_stretch = input_branch(
        tuple((swapped(grad_piece) for grad_piece in temporal_res[1:])),
        w_qkv_t,
        normed_mid,
        inverse_mid,
        modulation[3],
    )
    mid_grad = (out_grad.astype(jnp.float32) + temporal_branch).astype(jnp.bfloat16)
    arrived, landed = (
        lax.all_to_all(block_input, "seq", split_axis=0, concat_axis=1, tiled=True),
        lax.all_to_all(mid_grad, "seq", split_axis=0, concat_axis=1, tiled=True),
    )
    normed_fr, inverse_fr = layer_stats(arrived)
    frame_mod = modulate(normed_fr, modulation[0], modulation[1])
    frame_qkv = matmul_rows(frame_mod, w_qkv_s).astype(jnp.bfloat16)
    frame_cot = output_cot(landed, modulation[2], w_out_s)
    frame_res = attend(
        frame_qkv[..., :WIDTH],
        frame_qkv[..., WIDTH : 2 * WIDTH],
        frame_qkv[..., 2 * WIDTH :],
        frame_cot,
        qk_gain[0],
        qk_gain[1],
    )
    spatial_gate = gate_term(landed, frame_res[0], w_out_s)
    frame_branch, spatial_offset, spatial_stretch = input_branch(
        frame_res[1:], w_qkv_s, normed_fr, inverse_fr, modulation[1]
    )
    outgoing = frame_branch.astype(jnp.bfloat16)
    returned = lax.all_to_all(outgoing, "seq", split_axis=1, concat_axis=0, tiled=True)
    term_stack = jnp.stack(
        [
            spatial_offset,
            spatial_stretch,
            spatial_gate,
            temporal_offset,
            temporal_stretch,
            temporal_gate,
        ]
    )
    totals = lax.psum(term_stack, "seq")
    token_count = block_input.shape[0] * block_input.shape[1] * lax.axis_size("seq")
    mod_grad = totals * token_count ** (-0.5)
    input_grad = (mid_grad.astype(jnp.float32) + returned.astype(jnp.float32)).astype(jnp.bfloat16)
    return (input_grad, mod_grad)


def solution(mesh):
    return jax.shard_map(
        body,
        mesh=mesh,
        in_specs=(
            P("clip", "seq", None),
            P("clip", "seq", None),
            P(None, "clip", "seq", None),
            P("clip", "seq", None),
            P("clip", None),
            P(),
            P(),
            P(),
            P(),
            P(),
        ),
        out_specs=(P("clip", "seq", None), P("clip", None)),
        check_vma=False,
    )
```

profile of v0, /device:TPU:0, one launch (start us, length us, event | category | flops | bytes accessed | tf_op | source)
XLA Modules:
  0.0 314.7 jit_solution(16981990342659741506)
XLA Ops:
  0.7 7.6 %all-to-all-start = ((bf16[16,48,1152]{2,1,0:T(8,128)(2,1)}), bf16[16,48,1152]{2,1,0:T(8,128)(2,1)}, u32[]{:S(2)}, u32[]{:S(2)}) async-start(bf16[16,48,1152]{2,1,0:T(8,128)(2,1)} %param.10), calls=%async_computation | async-start | bytes 3538944 | tf_op jit(solution)/shard_map/all_to_all | solution.py:158
  12.2 3.8 %reshape.326 = bf16[48,16,8,72]{3,2,0,1:T(8,128)(2,1)} reshape(bf16[48,16,576]{2,0,1:T(8,128)(2,1)} %fusion.98) | data formatting | bytes 1769472 | tf_op jit(solution)/shard_map/reshape | solution.py:41
  16.0 3.8 %convert_bitcast_fusion.1 = (f32[48,16,576]{2,0,1:T(8,128)S(1)}, bf16[48,16,576]{2,0,1:T(8,128)(2,1)}, f32[48,16,576]{2,0,1:T(8,128)}) fusion(bf16[3,16,48,576]{3,2,1,0:T(8,128)(2,1)} %param.12), kind=kLoop, calls=%fused_computation.88 | loop fusion | flops 884736 | bytes 7077888 | tf_op jit(solution)/shard_map/convert_element_type | solution.py:45
  38.3 5.2 %fusion.94 = f32[48,8,16,16]{2,3,1,0:T(8,128)} fusion(bf16[48,16,8,72]{3,2,0,1:T(8,128)(2,1)S(1)} %copy-done.11, bf16[48,16,8,72]{3,2,0,1:T(8,128)(2,1)} %reshape.326), kind=kOutput, calls=%fused_computation.120 | convolution fusion | flops 14155776 | bytes 2162688 | tf_op jit(solution)/shard_map/blhd,bmhd->bhlm/dot_general | solution.py:74
  49.8 11.1 %fusion.38 = (f32[48,16,8]{1,2,0:T(8,128)}, f32[48,8,72,16]{2,3,1,0:T(8,128)}) fusion(f32[48,16,8,72]{3,2,1,0:T(8,128)} %reshape.338, f32[72]{0:T(128)S(1)} %copy-done.35, f32[48,8,16,16]{2,3,1,0:T(8,128)} %fusion.94, f32[48,8,16]{2,1,0:T(8,128)S(1)} %get-tuple-element.33, f32[48,8,16,16]{2,3,1,0:T(8,128)} %copy-done.19, f32[48,16,8,72]{3,2,1,0:T(8,128)} %reshape.337, ...), kind=kOutput, calls=%fused_computation.53 | convolution fusion | flops 17694736 | bytes 6169152 | tf_op jit(solution)/shard_map/bhlm,blhd->bmhd/dot_general | solution.py:85
  60.9 12.1 %fusion.41 = (f32[48,16,8]{1,2,0:T(8,128)}, f32[48,8,72,16]{2,3,1,0:T(8,128)}) fusion(f32[48,16,8,72]{3,2,1,0:T(8,128)} %reshape.337, f32[72]{0:T(128)S(1)} %copy-done.36, f32[48,8,16,16]{2,3,1,0:T(8,128)} %fusion.94, f32[48,8,16]{2,1,0:T(8,128)S(1)} %get-tuple-element.33, f32[48,8,16,16]{2,3,1,0:T(8,128)} %copy-done.19, f32[48,16,8,72]{3,2,1,0:T(8,128)} %reshape.338, ...), kind=kOutput, calls=%fused_computation.58 | convolution fusion | flops 17694736 | bytes 6169152 | tf_op jit(solution)/shard_map/bhlm,bmhd->blhd/dot_general | solution.py:82
  81.9 7.4 %fusion.37 = (bf16[48,16,8,72]{3,1,2,0:T(8,128)(2,1)S(1)}, bf16[48,16,8,72]{3,1,2,0:T(8,128)(2,1)S(1)}) fusion(f32[48,8,72,16]{2,3,1,0:T(8,128)} %get-tuple-element.38, f32[48,16,8,72]{3,2,1,0:T(8,128)} %reshape.338, f32[48,16,8]{1,2,0:T(8,128)} %copy.208, f32[48,16,8]{1,2,0:T(8,128)} %copy.204, f32[72]{0:T(128)S(1)} %copy-done.35, ...), kind=kLoop, calls=%fused_computation.52 | loop fusion | flops 5308416 | bytes 8995392 | tf_op jit(solution)/shard_map/convert_element_type | solution.py:55
  90.9 3.6 %reshape.329 = bf16[48,16,576]{2,1,0:T(8,128)(2,1)} reshape(bf16[48,16,8,72]{3,2,1,0:T(8,128)(2,1)} %copy.209) | data formatting | bytes 1769472 | tf_op jit(solution)/shard_map/reshape | solution.py:55
  96.1 3.8 %reshape.328 = bf16[48,16,576]{2,1,0:T(8,128)(2,1)} reshape(bf16[48,16,8,72]{3,2,1,0:T(8,128)(2,1)} %copy.203) | data formatting | bytes 1769472 | tf_op jit(solution)/shard_map/reshape | solution.py:55
  99.9 5.0 %concatenate.13 = bf16[16,48,1728]{2,0,1:T(8,128)(2,1)} concatenate(bf16[16,48,576]{2,0,1:T(8,128)(2,1)} %bitcast.185, bf16[16,48,576]{2,0,1:T(8,128)(2,1)S(1)} %bitcast.184, bf16[16,48,576]{2,0,1:T(8,128)(2,1)S(1)} %bitcast.183), dimensions={2} | concatenate | bytes 5308416 | tf_op jit(solution)/shard_map/concatenate | solution.py:108
  107.8 5.5 %fusion.138 = (f32[1152]{0:T(1024)S(1)}, f32[768]{0:T(1024)S(1)}, f32[768,1152]{1,0:T(8,128)}) fusion(f32[1152]{0:T(1024)S(1)} %copy-done.28, bf16[768,1728]{1,0:T(8,128)(2,1)S(1)} %bitcast.192, bf16[1152,1728]{0,1:T(8,128)(2,1)S(1)} %copy-done.38), kind=kOutput, calls=%fused_computation.175 | convolution fusion | flops 3060300032 | bytes 10186752 | tf_op jit(solution)/shard_map/dot_general | solution.py:34
  119.2 6.2 %all-to-all-start.1 = ((bf16[16,48,1152]{2,1,0:T(8,128)(2,1)}), bf16[16,48,1152]{2,1,0:T(8,128)(2,1)}, u32[]{:S(2)}, u32[]{:S(2)}) async-start(bf16[16,48,1152]{2,1,0:T(8,128)(2,1)} %fusion.26), calls=%async_computation.1 | async-start | bytes 3538944 | tf_op jit(solution)/shard_map/all_to_all | solution.py:159
  133.4 3.8 %fusion.33 = bf16[2,384,1728]{1,2,0:T(8,128)(2,1)S(1)} fusion(bf16[2,384,1152]{2,1,0:T(8,128)(2,1)S(1)} %add_convert_fusion, bf16[1152,1728]{0,1:T(8,128)(2,1)S(1)} %copy-done.39), kind=kOutput, calls=%fused_computation.47 | convolution fusion | flops 3058974720 | bytes 8404992 | tf_op jit(solution)/shard_map/dot_general | solution.py:28
  139.0 27.2 %all-to-all-done.1 = bf16[16,48,1152]{2,1,0:T(8,128)(2,1)} async-done(((bf16[16,48,1152]{2,1,0:T(8,128)(2,1)}), bf16[16,48,1152]{2,1,0:T(8,128)(2,1)}, u32[]{:S(2)}, u32[]{:S(2)}) %all-to-all-start.1) | async-done | bytes 1769504 | tf_op jit(solution)/shard_map/all_to_all | solution.py:159
  171.6 5.1 %fusion.148 = f32[2,8,384,384]{2,3,1,0:T(8,128)} fusion(bf16[2,384,8,72]{1,3,2,0:T(8,128)(2,1)S(1)} %bitcast.197, bf16[2,384,8,72]{1,3,2,0:T(8,128)(2,1)S(1)} %bitcast.190), kind=kOutput, calls=%fused_computation.178 | convolution fusion | flops 339738624 | bytes 11206656 | tf_op jit(solution)/shard_map/blhd,bmhd->bhlm/dot_general | solution.py:74
  178.7 3.6 %copy-done.10 = f32[2,8,384,384]{2,3,1,0:T(8,128)} copy-done((f32[2,8,384,384]{2,3,1,0:T(8,128)}, f32[2,8,384,384]{2,3,1,0:T(8,128)S(1)}, u32[]{:S(2)}) %copy-start.10) | copy-done | bytes 9437208
  185.3 18.2 %fusion.63 = (f32[2,384,8]{1,2,0:T(8,128)S(1)}, f32[2,8,72,384]{3,2,1,0:T(8,128)}) fusion(bf16[2,384,8,72]{1,3,2,0:T(8,128)(2,1)S(1)} %bitcast.175, f32[72]{0:T(128)S(1)} %copy-done.33, f32[2,8,384,384]{2,3,1,0:T(8,128)} %fusion.148, f32[2,8,384]{2,1,0:T(8,128)S(1)} %get-tuple-element.40, f32[2,8,384,384]{2,3,1,0:T(8,128)} %copy-done.10, ...), kind=kOutput, calls=%fused_computation.95 | convolution fusion | flops 364511616 | bytes 22487616 | tf_op jit(solution)/shard_map/bhlm,blhd->bmhd/dot_general | solution.py:85
  203.5 17.9 %fusion.70 = (f32[2,384,8]{1,2,0:T(8,128)S(1)}, f32[2,8,72,384]{3,2,1,0:T(8,128)}) fusion(bf16[2,384,8,72]{1,3,2,0:T(8,128)(2,1)S(1)} %bitcast.181, f32[72]{0:T(128)S(1)} %copy-done.34, f32[2,8,384,384]{2,3,1,0:T(8,128)} %fusion.148, f32[2,8,384]{2,1,0:T(8,128)S(1)} %get-tuple-element.40, f32[2,8,384,384]{2,3,1,0:T(8,128)} %copy-done.10, ...), kind=kOutput, calls=%fused_computation.102 | convolution fusion | flops 364511616 | bytes 22487616 | tf_op jit(solution)/shard_map/bhlm,bmhd->blhd/dot_general | solution.py:82
  228.4 6.2 %multiply_reduce_fusion.1 = (f32[1152]{0:T(1024)S(1)}, f32[768]{0:T(1024)S(1)}, f32[768]{0:T(1024)S(1)}, f32[1152]{0:T(1024)S(1)}, f32[768,1152]{1,0:T(8,128)}) fusion(f32[8,2,48,1152]{3,2,0,1:T(8,128)S(1)} %copy-done.4, f32[768]{0:T(1024)S(1)} %rsqrt.74, f32[768]{0:T(1024)S(1)} %div.96, f32[1152]{0:T(1024)S(1)} %copy-done.29, ...), kind=kOutput, calls=%fused_computation.42 | convolution fusion | flops 3073569280 | bytes 13739520 | tf_op jit(solution)/shard_map/dot_general | solution.py:34
  234.6 3.9 %multiply_convert_fusion.1 = bf16[2,384,1152]{2,1,0:T(8,128)(2,1)S(1)} fusion(f32[2,384,1152]{2,1,0:T(8,128)} %bitcast.189, f32[8,2,48,1152]{3,2,0,1:T(8,128)} %copy-done.3, f32[2,384]{1,0:T(2,128)S(1)} %div.98, f32[2,384]{1,0:T(2,128)S(1)} %div.95, f32[1152]{0:T(1024)S(1)} %copy-done.29, f32[2,384]{1,0:T(2,128)S(1)} %div.87, f32[2,384]{1,0:T(2,128)S(1)} %rsqrt.71), kind=kLoop, calls=%fused_computation.43 | loop fusion | flops 7077888 | bytes 8864256 | tf_op jit(solution)/shard_map/convert_element_type | solution.py:177
  241.7 4.3 %all-to-all-start.2 = ((bf16[2,384,1152]{2,0,1:T(2,128)(2,1)}), bf16[2,384,1152]{2,0,1:T(2,128)(2,1)}, u32[]{:S(2)}, u32[]{:S(2)}) async-start(bf16[2,384,1152]{2,0,1:T(2,128)(2,1)} %copy.221), calls=%async_computation.2 | async-start | bytes 3538944 | tf_op jit(solution)/shard_map/all_to_all | solution.py:178
  251.8 3.5 %fusion.81 = f32[1152]{0:T(1024)S(1)} fusion(bf16[16,48,1152]{2,1,0:T(8,128)(2,1)} %param.13, bf16[576,1152]{1,0:T(8,128)(2,1)S(1)} %copy-done, bf16[16,48,576]{2,0,1:T(8,128)(2,1)} %bitcast.193), kind=kOutput, calls=%fused_computation.112 | convolution fusion | flops 1021868928 | bytes 3985920 | tf_op jit(solution)/shard_map/dot_general | solution.py:28
  255.3 5.6 %fusion.90 = bf16[2,8,72,384]{3,2,1,0:T(8,128)(2,1)S(1)} fusion(bf16[2,384,8,72]{1,3,2,0:T(8,128)(2,1)S(1)} %bitcast.191, f32[2,8,384,384]{2,3,1,0:T(8,128)} %copy-done.10, f32[2,8,384]{2,1,0:T(8,128)S(1)} %get-tuple-element.40), kind=kOutput, calls=%fused_computation.117 | convolution fusion | flops 347258880 | bytes 11231232 | tf_op jit(solution)/shard_map/bhlm,bmhd->blhd/dot_general | solution.py:71
  262.8 47.5 %psum.7 = f32[6,1152]{1,0:T(8,128)S(1)} all-reduce(f32[6,1152]{1,0:T(8,128)S(1)} %stack.27), channel_id=1, replica_groups=mesh['clip'=4,'seq'=8] {'seq'}, use_global_device_ids=true, to_apply=%region_26.0 | all-reduce | flops 6912 | bytes 55296 | tf_op jit(solution)/shard_map/psum | solution.py:189
  (176 shorter events, 90.9 us)
Async XLA Ops:
  0.6 8.9 %copy-start = (bf16[576,1152]{1,0:T(8,128)(2,1)S(1)}, bf16[576,1152]{1,0:T(8,128)(2,1)}, u32[]{:S(2)}) copy-start(bf16[576,1152]{1,0:T(8,128)(2,1)} %param.18) | copy-start | bytes 3981316
  0.6 7.6 %copy-start.37 = (f32[4,72]{1,0:T(4,128)S(1)}, f32[4,72]{1,0:T(4,128)}, u32[]{:S(2)}) copy-start(f32[4,72]{1,0:T(4,128)} %param.19) | copy-start | bytes 3460
  0.7 8.2 %copy-start.32 = (f32[5,1152]{1,0:T(8,128)S(1)}, f32[5,1152]{1,0:T(8,128)}, u32[]{:S(2)}) copy-start(f32[5,1152]{1,0:T(8,128)} %param.14) | copy-start | bytes 69124
  0.7 8.8 %copy-start.20 = (bf16[16,48,1152]{2,1,0:T(8,128)(2,1)S(1)}, bf16[16,48,1152]{2,1,0:T(8,128)(2,1)}, u32[]{:S(2)}) copy-start(bf16[16,48,1152]{2,1,0:T(8,128)(2,1)} %param.13) | copy-start | bytes 5308420
  0.7 118.6 %all-to-all-start = ((bf16[16,48,1152]{2,1,0:T(8,128)(2,1)}), bf16[16,48,1152]{2,1,0:T(8,128)(2,1)}, u32[]{:S(2)}, u32[]{:S(2)}) async-start(bf16[16,48,1152]{2,1,0:T(8,128)(2,1)} %param.10), calls=%async_computation | async-start | bytes 3538944 | tf_op jit(solution)/shard_map/all_to_all | solution.py:158
  34.4 3.9 %copy-start.11 = (bf16[48,16,8,72]{3,2,0,1:T(8,128)(2,1)S(1)}, bf16[48,16,8,72]{3,2,0,1:T(8,128)(2,1)}, u32[]{:S(2)}) copy-start(bf16[48,16,8,72]{3,2,0,1:T(8,128)(2,1)} %reshape.355) | copy-start | bytes 2654212
  38.3 5.2 %copy-start.1 = (f32[48,16,8,72]{3,2,1,0:T(8,128)S(1)}, f32[48,16,8,72]{3,2,1,0:T(8,128)}, u32[]{:S(2)}) copy-start(f32[48,16,8,72]{3,2,1,0:T(8,128)} %reshape.337) | copy-start | bytes 5308420
  38.3 5.2 %copy-start.2 = (f32[48,16,8,72]{3,2,1,0:T(8,128)S(1)}, f32[48,16,8,72]{3,2,1,0:T(8,128)}, u32[]{:S(2)}) copy-start(f32[48,16,8,72]{3,2,1,0:T(8,128)} %reshape.338) | copy-start | bytes 5308420
  38.3 5.2 %copy-start.35 = (f32[72]{0:T(128)S(1)}, f32[72]{0:T(128)}, u32[]{:S(2)}) copy-start(f32[72]{0:T(128)} %get-tuple-element.30) | copy-start | bytes 868
  38.3 5.2 %copy-start.36 = (f32[72]{0:T(128)S(1)}, f32[72]{0:T(128)}, u32[]{:S(2)}) copy-start(f32[72]{0:T(128)} %get-tuple-element.31) | copy-start | bytes 868
  45.6 15.3 %copy-start.26 = (f32[48,8,16]{2,1,0:T(8,128)}, f32[48,8,16]{2,1,0:T(8,128)S(1)}, u32[]{:S(2)}) copy-start(f32[48,8,16]{2,1,0:T(8,128)S(1)} %get-tuple-element.33) | copy-start | bytes 73732
  60.9 12.1 %copy-start.24 = (f32[48,16,8]{0,2,1:T(8,128)S(1)}, f32[48,16,8]{0,2,1:T(8,128)}, u32[]{:S(2)}) copy-start(f32[48,16,8]{0,2,1:T(8,128)} %get-tuple-element.23) | copy-start | bytes 73732
  60.9 12.3 %copy-start.25 = (f32[48,16,8]{0,2,1:T(8,128)S(1)}, f32[48,16,8]{0,2,1:T(8,128)}, u32[]{:S(2)}) copy-start(f32[48,16,8]{0,2,1:T(8,128)} %get-tuple-element.21) | copy-start | bytes 73732
  107.8 5.6 %copy-start.5 = (bf16[16,48,1152]{2,1,0:T(8,128)(2,1)S(1)}, bf16[16,48,1152]{2,1,0:T(8,128)(2,1)}, u32[]{:S(2)}) copy-start(bf16[16,48,1152]{2,1,0:T(8,128)(2,1)} %param.11) | copy-start | bytes 5308420
  119.2 46.9 %all-to-all-start.1 = ((bf16[16,48,1152]{2,1,0:T(8,128)(2,1)}), bf16[16,48,1152]{2,1,0:T(8,128)(2,1)}, u32[]{:S(2)}, u32[]{:S(2)}) async-start(bf16[16,48,1152]{2,1,0:T(8,128)(2,1)} %fusion.26), calls=%async_computation.1 | async-start | bytes 3538944 | tf_op jit(solution)/shard_map/all_to_all | solution.py:159
  138.7 29.2 %copy-start.30 = (f32[1152]{0:T(1024)S(1)}, f32[1152]{0:T(1024)}, u32[]{:S(2)}) copy-start(f32[1152]{0:T(1024)} %get-tuple-element.13) | copy-start | bytes 13828
  171.6 5.1 %copy-start.33 = (f32[72]{0:T(128)S(1)}, f32[72]{0:T(128)}, u32[]{:S(2)}) copy-start(f32[72]{0:T(128)} %get-tuple-element.29) | copy-start | bytes 868
  171.6 5.1 %copy-start.34 = (f32[72]{0:T(128)S(1)}, f32[72]{0:T(128)}, u32[]{:S(2)}) copy-start(f32[72]{0:T(128)} %get-tuple-element.32) | copy-start | bytes 868
  238.5 7.5 %copy-start.12 = (bf16[48,16,8,72]{3,2,0,1:T(8,128)(2,1)S(1)}, bf16[48,16,8,72]{3,2,0,1:T(8,128)(2,1)}, u32[]{:S(2)}) copy-start(bf16[48,16,8,72]{3,2,0,1:T(8,128)(2,1)} %reshape.355) | copy-start | bytes 2654212
  238.5 7.5 %copy-start.27 = (f32[48,8,16]{2,1,0:T(8,128)S(1)}, f32[48,8,16]{2,1,0:T(8,128)}, u32[]{:S(2)}) copy-start(f32[48,8,16]{2,1,0:T(8,128)} %copy-done.26) | copy-start | bytes 73732
  241.7 69.3 %all-to-all-start.2 = ((bf16[2,384,1152]{2,0,1:T(2,128)(2,1)}), bf16[2,384,1152]{2,0,1:T(2,128)(2,1)}, u32[]{:S(2)}, u32[]{:S(2)}) async-start(bf16[2,384,1152]{2,0,1:T(2,128)(2,1)} %copy.221), calls=%async_computation.2 | async-start | bytes 3538944 | tf_op jit(solution)/shard_map/all_to_all | solution.py:178
  255.3 5.6 %copy-start.9 = (f32[8,2,48,1152]{3,2,0,1:T(8,128)S(1)}, f32[8,2,48,1152]{3,2,0,1:T(8,128)}, u32[]{:S(2)}) copy-start(f32[8,2,48,1152]{3,2,0,1:T(8,128)} %copy-done.8) | copy-start | bytes 10616836
  255.3 5.6 %copy-start.42 = (bf16[576,1152]{1,0:T(8,128)(2,1)S(1)}, bf16[576,1152]{1,0:T(8,128)(2,1)}, u32[]{:S(2)}) copy-start(bf16[576,1152]{1,0:T(8,128)(2,1)} %param.16) | copy-start | bytes 3981316
  262.7 50.0 %copy-start.6 = (bf16[16,48,1152]{2,1,0:T(8,128)(2,1)S(1)}, bf16[16,48,1152]{2,1,0:T(8,128)(2,1)}, u32[]{:S(2)}) copy-start(bf16[16,48,1152]{2,1,0:T(8,128)(2,1)} %fusion.26) | copy-start | bytes 5308420
  (22 other events, 64.2 us)
where the time goes:
time: 321 us; the launch traced here: 315 us
  matrix products  113 us (35%)
  local copies, waits for them, and re-layouts  72.6 us (23%)
  blocking collectives  47.5 us (15%)
  other arithmetic  34.5 us (11%)
  waiting for transfers between devices  27.2 us (8%)
  starting transfers between devices  18.1 us (6%)
    psum x1, blocking collectives, body(): totals = lax.psum(term_stack, 'seq')  47.5 us
    dot_general x2, matrix products, attend(): jnp.einsum('bhlm,bmhd->blhd', score_grad, key_norm, preferred_element_typ...  30 us
    dot_general x2, matrix products, attend(): jnp.einsum('bhlm,blhd->bmhd', score_grad, query_norm, preferred_element_t...  29.3 us
    all_to_all x1, waiting for transfers between devices, body(): lax.all_to_all(mid_grad, 'seq', split_axis=0, concat_axis=1, tiled=True)  27.2 us
    dot_general x4, matrix products, matmul_back(): lax.dot_general(flattened, weight, (((1,), (1,)), ((), ())), preferred_el...  15.7 us
    unnamed x89, local copies, waits for them, and re-layouts  13.3 us
    dot_general x2, matrix products, attend(): jnp.einsum('blhd,bmhd->bhlm', cot_heads, value_heads, preferred_element_t...  10.3 us
    dot_general x3, matrix products, matmul_rows(): result = jnp.dot(flattened, weight, preferred_element_type=jnp.float32)  9.04 us
  transfers between devices with their start and end apart: 3, of which 1 were waited for; matrix products, arithmetic and copies ran while one was open for 43% of the time, Pallas kernels for 0%

commit v1 on v0

v1 whole, which is shorter than its diff:
```python
import functools
import math

import jax
import jax.numpy as jnp
from jax import lax
from jax.experimental import pallas as pl
from jax.experimental.pallas import tpu as pltpu
from jax.sharding import PartitionSpec as P

HEAD_DIM = 72
NORM_EPS = 1e-06
LANES = 128
GROUP = 8
F32 = jnp.float32
BF16 = jnp.bfloat16


def nt(a, b):
    return lax.dot_general(a, b, (((1,), (1,)), ((), ())), preferred_element_type=F32)


def nn(a, b):
    return lax.dot_general(a, b, (((1,), (0,)), ((), ())), preferred_element_type=F32)


def tn(a, b):
    return lax.dot_general(a, b, (((0,), (0,)), ((), ())), preferred_element_type=F32)


def windows(width):
    pairs = width // (2 * HEAD_DIM)
    return [(LANES * p, min(2 * LANES, width - LANES * p), 2 * HEAD_DIM * p - LANES * p) for p in range(pairs)]


def attention_pair(q, k, v, c, gain_q, gain_k, first, same):
    rows, lanes = q.shape
    lane = lax.broadcasted_iota(jnp.int32, (1, lanes), 1)
    in0 = jnp.logical_and(lane >= first, lane < first + HEAD_DIM)
    in1 = jnp.logical_and(lane >= first + HEAD_DIM, lane < first + 2 * HEAD_DIM)
    m0, m1 = in0.astype(F32), in1.astype(F32)
    b0, b1 = m0.astype(BF16), m1.astype(BF16)

    def head_mean(t):
        mean0 = jnp.sum(t * m0, axis=-1, keepdims=True) * (1.0 / HEAD_DIM)
        mean1 = jnp.sum(t * m1, axis=-1, keepdims=True) * (1.0 / HEAD_DIM)
        return mean0, mean1

    def norm(t):
        mean0, mean1 = head_mean(t * t)
        return lax.rsqrt(mean0 + NORM_EPS) * m0 + lax.rsqrt(mean1 + NORM_EPS) * m1

    def both(t):
        return jnp.concatenate([t * b0, t * b1], axis=0)

    def stacked(t):
        return jnp.concatenate([t[:, :rows], t[:, rows:]], axis=0)

    rq, rk = norm(q), norm(k)
    qn = (q * rq * gain_q).astype(BF16)
    kn = (k * rk * gain_k).astype(BF16)
    vb, cb = v.astype(BF16), c.astype(BF16)
    k2, v2, q2, c2 = both(kn), both(vb), both(qn), both(cb)
    factor = HEAD_DIM**-0.5
    e = jnp.exp2(nt(qn, k2) * (factor / math.log(2.0)))
    if same is not None:
        e = jnp.where(jnp.concatenate([same, same], axis=1), e, 0.0)
    dp = nt(cb, v2)
    ps, dss = [], []
    for h in range(2):
        eh, dph = e[:, h * rows : (h + 1) * rows], dp[:, h * rows : (h + 1) * rows]
        p = eh * (1.0 / jnp.sum(eh, axis=-1, keepdims=True))
        inner = jnp.sum(p * dph, axis=-1, keepdims=True)
        dss.append((p * (dph - inner)).astype(BF16))
        ps.append(p.astype(BF16))
    o = nn(jnp.concatenate(ps, axis=1), v2)
    gv = tn(jnp.concatenate(ps, axis=0), c2)
    eq = nn(jnp.concatenate(dss, axis=1), k2)
    ek = tn(jnp.concatenate(dss, axis=0), q2)

    def norm_back(raw, inverse, gain, upstream):
        scaled = (gain * factor) * upstream
        mean0, mean1 = head_mean(raw * scaled)
        return inverse * scaled - raw * (inverse * inverse * inverse) * (mean0 * m0 + mean1 * m1)

    return o, norm_back(q, rq, gain_q, eq), norm_back(k, rk, gain_k, ek), gv


def merge(parts, width):
    columns = []
    for p in range(len(parts)):
        low = parts[p][:, :LANES]
        columns.append(low if p == 0 else low + parts[p - 1][:, LANES:])
    columns.append(parts[-1][:, LANES:])
    return jnp.concatenate(columns, axis=1)[:, :width]


def layer_norm(u):
    centre = jnp.mean(u, axis=-1, keepdims=True)
    delta = u - centre
    inverse = lax.rsqrt(jnp.mean(delta * delta, axis=-1, keepdims=True) + NORM_EPS)
    return delta * inverse, inverse


def branch_of(gm, normed, inverse, stretch):
    gn = gm * (1.0 + stretch)
    return inverse * (
        gn - jnp.mean(gn, axis=-1, keepdims=True) - normed * jnp.mean(gn * normed, axis=-1, keepdims=True)
    )


def temporal_kernel(qkv, og, u, mod, gains, w_out, w_qkv, y, sums, c_s, o_s, g_s, gm_s, ow_s):
    frames, tokens, d = og.shape
    width = w_out.shape[0]
    rows = frames * tokens
    a_s, a_g = mod[3:4, :], mod[4:5, :]

    yb = (og[...].astype(F32).reshape(rows, d) * a_g).astype(BF16)
    c_s[...] = nt(yb, w_out[...]).astype(BF16).astype(F32).reshape(frames, tokens, width)

    n = frames * GROUP
    ri = lax.broadcasted_iota(jnp.int32, (n, n), 0)
    ci = lax.broadcasted_iota(jnp.int32, (n, n), 1)
    same = (ri & (GROUP - 1)) == (ci & (GROUP - 1))

    def group(g, carry):
        at = pl.ds(pl.multiple_of(g * GROUP, GROUP), GROUP)
        outs = []
        for start, lanes, first in windows(width):
            w = pl.ds(start, lanes)
            q = qkv[0, :, at, w].astype(F32).reshape(n, lanes)
            k = qkv[1, :, at, w].astype(F32).reshape(n, lanes)
            v = qkv[2, :, at, w].astype(F32).reshape(n, lanes)
            c = c_s[:, at, w].reshape(n, lanes)
            outs.append(attention_pair(q, k, v, c, gains[2:3, w], gains[3:4, w], first, same))
        o, gq, gk, gv = [merge([t[x] for t in outs], width) for x in range(4)]
        o_s[:, at, :] = o.reshape(frames, GROUP, width)
        g_s[:, at, 0:width] = gq.reshape(frames, GROUP, width)
        g_s[:, at, width : 2 * width] = gk.reshape(frames, GROUP, width)
        g_s[:, at, 2 * width : 3 * width] = gv.reshape(frames, GROUP, width)
        return carry

    lax.fori_loop(0, tokens // GROUP, group, 0)

    ow_s[...] = nn(o_s[...].astype(BF16).reshape(rows, width), w_out[...]).reshape(frames, tokens, d)
    gm_s[...] = nt(g_s[...].astype(BF16).reshape(rows, 3 * width), w_qkv[...]).reshape(frames, tokens, d)

    def tail(f, carry):
        shift, scale, gate = carry
        y0 = og[f].astype(F32)
        normed, inverse = layer_norm(u[f].astype(F32))
        gm = gm_s[f]
        y[f] = (y0 + branch_of(gm, normed, inverse, a_s)).astype(BF16)
        return (
            shift + jnp.sum(gm, axis=0, keepdims=True),
            scale + jnp.sum(gm * normed, axis=0, keepdims=True),
            gate + jnp.sum(y0 * ow_s[f], axis=0, keepdims=True),
        )

    zero = jnp.zeros((1, d), F32)
    shift, scale, gate = lax.fori_loop(0, frames, tail, (zero, zero, zero))
    sums[0:1, :] = shift
    sums[1:2, :] = scale
    sums[2:3, :] = gate


def temporal(saved_qkv, out_grad, mid_state, modulation, gains, w_out, w_qkv):
    frames, tokens, d = out_grad.shape
    width = w_out.shape[0]
    vm = pl.BlockSpec(memory_space=pltpu.VMEM)
    flops = 2 * frames * tokens * d * width * 5
    return pl.pallas_call(
        temporal_kernel,
        out_shape=(jax.ShapeDtypeStruct(out_grad.shape, BF16), jax.ShapeDtypeStruct((3, d), F32)),
        in_specs=[vm] * 7,
        out_specs=(vm, vm),
        scratch_shapes=[
            pltpu.VMEM((frames, tokens, width), F32),
            pltpu.VMEM((frames, tokens, width), F32),
            pltpu.VMEM((frames, tokens, 3 * width), F32),
            pltpu.VMEM((frames, tokens, d), F32),
            pltpu.VMEM((frames, tokens, d), F32),
        ],
        compiler_params=pltpu.CompilerParams(vmem_limit_bytes=60 << 20),
        cost_estimate=pl.CostEstimate(flops=flops * 2, bytes_accessed=12 << 20, transcendentals=0),
        name="temporal",
    )(saved_qkv, out_grad, mid_state, modulation, gains, w_out, w_qkv)


def project_kernel(x, mod, w_qkv, q, k, v):
    src, _, tokens, d = x.shape
    width = q.shape[-1]
    normed, _ = layer_norm(x[...].astype(F32).reshape(src * tokens, d))
    m = (normed * (1.0 + mod[1:2, :]) + mod[0:1, :]).astype(BF16)
    qkv = nn(m, w_qkv[...]).astype(BF16)
    q[0] = qkv[:, :width]
    k[0] = qkv[:, width : 2 * width]
    v[0] = qkv[:, 2 * width :]


def project(x, modulation, w_qkv):
    src, frames, tokens, d = x.shape
    width = w_qkv.shape[1] // 3
    rows = src * tokens
    out = jax.ShapeDtypeStruct((frames, rows, width), BF16)
    block = pl.BlockSpec((1, rows, width), lambda f: (f, 0, 0))
    return pl.pallas_call(
        project_kernel,
        grid=(frames,),
        out_shape=(out, out, out),
        in_specs=[
            pl.BlockSpec((src, 1, tokens, d), lambda f: (0, f, 0, 0)),
            pl.BlockSpec(modulation.shape, lambda f: (0, 0)),
            pl.BlockSpec(w_qkv.shape, lambda f: (0, 0)),
        ],
        out_specs=(block, block, block),
        compiler_params=pltpu.CompilerParams(vmem_limit_bytes=60 << 20),
        cost_estimate=pl.CostEstimate(
            flops=2 * frames * rows * d * 3 * width, bytes_accessed=8 << 20, transcendentals=0
        ),
        name="project",
    )(x, modulation, w_qkv)


def spatial_kernel(x, y, q, k, v, mod, gains, w_out, w_qkv, b, sums, g_s):
    src, _, tokens, d = x.shape
    width = w_out.shape[0]
    rows = src * tokens
    a_s, a_g = mod[1:2, :], mod[2:3, :]
    yf = y[...].astype(F32).reshape(rows, d)
    c = nt((yf * a_g).astype(BF16), w_out[...]).astype(BF16).astype(F32)
    outs = []
    for start, lanes, first in windows(width):
        w = pl.ds(start, lanes)
        args = [t[0, :, w].astype(F32) for t in (q, k, v)]
        outs.append(
            attention_pair(*args, c[:, start : start + lanes], gains[0:1, w], gains[1:2, w], first, None)
        )
    o, gq, gk, gv = [merge([t[i] for t in outs], width).astype(BF16) for i in range(4)]
    g_s[:, 0:width] = gq
    g_s[:, width : 2 * width] = gk
    g_s[:, 2 * width : 3 * width] = gv
    sums[2:3, :] = jnp.sum(yf * nn(o, w_out[...]), axis=0, keepdims=True)
    gm = nt(g_s[...], w_qkv[...])
    normed, inverse = layer_norm(x[...].astype(F32).reshape(rows, d))
    sums[0:1, :] = jnp.sum(gm, axis=0, keepdims=True)
    sums[1:2, :] = jnp.sum(gm * normed, axis=0, keepdims=True)
    b[...] = branch_of(gm, normed, inverse, a_s).reshape(src, tokens, d).astype(BF16)


def spatial(f, x, y, q, k, v, modulation, gains, w_out, w_qkv):
    src, _, tokens, d = x.shape
    width = w_out.shape[0]
    rows = src * tokens
    head = pl.BlockSpec((1, rows, width), lambda i: (f, 0, 0))
    token = pl.BlockSpec((src, 1, tokens, d), lambda i: (0, f, 0, 0))

    def whole(a):
        return pl.BlockSpec(a.shape, lambda i: (0,) * a.ndim)

    flops = 2 * rows * d * width * 5 + 12 * rows * rows * width
    return pl.pallas_call(
        spatial_kernel,
        grid=(1,),
        out_shape=(jax.ShapeDtypeStruct((src, tokens, d), BF16), jax.ShapeDtypeStruct((3, d), F32)),
        in_specs=[token, token, head, head, head]
        + [whole(a) for a in (modulation, gains, w_out, w_qkv)],
        out_specs=(
            pl.BlockSpec((src, tokens, d), lambda i: (0, 0, 0)),
            pl.BlockSpec((3, d), lambda i: (0, 0)),
        ),
        scratch_shapes=[pltpu.VMEM((rows, 3 * width), BF16)],
        compiler_params=pltpu.CompilerParams(vmem_limit_bytes=60 << 20),
        cost_estimate=pl.CostEstimate(flops=flops * 2, bytes_accessed=8 << 20, transcendentals=0),
        name="spatial",
    )(x, y, q, k, v, modulation, gains, w_out, w_qkv)


def reduce_all(t, size):
    step = size // 2
    while step:
        t = t + lax.ppermute(t, "seq", [(i, i ^ step) for i in range(size)])
        step //= 2
    return t


def exchange(t):
    return lax.all_to_all(t, "seq", split_axis=0, concat_axis=0, tiled=True)


def body(size, block_input, mid_state, saved_qkv, out_grad, modulation, w_qkv_s, w_out_s, w_qkv_t, w_out_t, qk_gain):
    frames, tokens, d = out_grad.shape
    per = frames // size
    heads = w_out_t.shape[0] // HEAD_DIM
    gains = jnp.tile(qk_gain, (1, heads))
    x = exchange(block_input).reshape(size, per, tokens, d)
    y, sums_t = temporal(saved_qkv, out_grad, mid_state, modulation, gains, w_out_t, w_qkv_t)
    landed = exchange(y).reshape(size, per, tokens, d)
    q, k, v = project(x, modulation, w_qkv_s)
    results = [spatial(f, x, landed, q, k, v, modulation, gains, w_out_s, w_qkv_s) for f in range(per)]
    outgoing = jnp.stack([r[0] for r in results], axis=1).reshape(frames, tokens, d)
    returned = exchange(outgoing)
    sums_s = sum(r[1] for r in results)
    totals = reduce_all(jnp.concatenate([sums_s, sums_t], axis=0), size)
    token_count = frames * tokens * size
    input_grad = (y.astype(F32) + returned.astype(F32)).astype(BF16)
    return input_grad, totals * token_count ** (-0.5)


def solution(mesh):
    return jax.shard_map(
        functools.partial(body, mesh.shape["seq"]),
        mesh=mesh,
        in_specs=(
            P("clip", "seq", None),
            P("clip", "seq", None),
            P(None, "clip", "seq", None),
            P("clip", "seq", None),
            P("clip", None),
            P(),
            P(),
            P(),
            P(),
            P(),
        ),
        out_specs=(P("clip", "seq", None), P("clip", None)),
        check_vma=False,
    )
```

time: 321 us -> 187 us (0.58); the launches traced: 315 us -> 187 us
  matrix products: 113 us -> 0 us
  Pallas kernels: 0 us -> 68.6 us
  local copies, waits for them, and re-layouts: 72.6 us -> 17.4 us
  waiting for transfers between devices: 27.2 us -> 75 us
  blocking collectives: 47.5 us -> 0 us
  other arithmetic: 34.5 us -> 5.82 us
    dot_general x19 -> x0, matrix products: 113 us -> none  [the longest x2 30 us: attend(): jnp.einsum('bhlm,bmhd->blhd', score_grad, key_norm, preferred_element_typ...]
    pallas_call x0 -> x4, Pallas kernels: none -> 68.6 us  [the longest x1 31 us: temporal(): pl.pallas_call(temporal_kernel, out_shape=(jax.ShapeDtypeStruct(out_grad....]
    psum x1 -> x0, blocking collectives: 47.5 us -> none  [body(): totals = lax.psum(term_stack, 'seq')]
    ppermute x0 -> x3, waiting for transfers between devices: none -> 44.9 us  [reduce_all(): t = t + lax.ppermute(t, 'seq', [(i, i ^ step) for i in range(size)])]
    convert_element_type x15 -> x0, local copies, waits for them, and re-layouts: 25.9 us -> none  [the longest x4 8.23 us: rms_normed(): values = head_split(raw_rows).astype(jnp.float32)]
    convert_element_type x10 -> x1, other arithmetic: 22.7 us -> 1.63 us  [body(): input_grad = (y.astype(F32) + returned.astype(F32)).astype(BF16)]
    reshape x6 -> x0, local copies, waits for them, and re-layouts: 18.2 us -> none  [the longest x2 7.43 us: rms_back(): return result.astype(jnp.bfloat16).reshape(values.shape[:-2] + (-1,))]
    reduce_sum x9 -> x0, other arithmetic: 9.18 us -> none  [the longest x4 6.2 us: rms_normed(): jnp.mean(values * values, axis=-1, keepdims=True) + NORM_EPS]
  transfers between devices with their start and end apart: 3 -> 6, of which waited for: 1 -> 5; matrix products, arithmetic and copies ran while one was open for 43% -> 9% of each run, Pallas kernels for 0% -> 21%
where the time goes in v1:
time: 187 us
  waiting for transfers between devices  75 us (40%)
  Pallas kernels  68.6 us (37%)
  starting transfers between devices  19.2 us (10%)
  local copies, waits for them, and re-layouts  17.4 us (9%)
  other arithmetic  5.82 us (3%)
    ppermute x3, waiting for transfers between devices, reduce_all(): t = t + lax.ppermute(t, 'seq', [(i, i ^ step) for i in range(size)])  44.9 us
    pallas_call x1, Pallas kernels, temporal(): pl.pallas_call(temporal_kernel, out_shape=(jax.ShapeDtypeStruct(out_grad....  31 us
    all_to_all x3, waiting for transfers between devices, exchange(): return lax.all_to_all(t, 'seq', split_axis=0, concat_axis=0, tiled=True)  30 us
    pallas_call x2, Pallas kernels, spatial(): pl.pallas_call(spatial_kernel, grid=(1,), out_shape=(jax.ShapeDtypeStruct...  29.6 us
    unnamed x12, local copies, waits for them, and re-layouts  15.3 us
    all_to_all x3, starting transfers between devices, exchange(): return lax.all_to_all(t, 'seq', split_axis=0, concat_axis=0, tiled=True)  14.7 us
    pallas_call x1, Pallas kernels, project(): pl.pallas_call(project_kernel, grid=(frames,), out_shape=(out, out, out),...  7.96 us
    ppermute x3, starting transfers between devices, reduce_all(): t = t + lax.ppermute(t, 'seq', [(i, i ^ step) for i in range(size)])  4.52 us
  transfers between devices with their start and end apart: 6, of which 5 were waited for; matrix products, arithmetic and copies ran while one was open for 9% of the time, Pallas kernels for 21%

profile of v1, /device:TPU:0, one launch (start us, length us, event | category | flops | bytes accessed | tf_op | source)
XLA Modules:
  0.0 186.6 jit_solution(50736695196216851)
XLA Ops:
  0.6 7.3 %all-to-all-start = ((bf16[16,48,1152]{2,1,0:T(8,128)(2,1)}), bf16[16,48,1152]{2,1,0:T(8,128)(2,1)S(1)}, u32[]{:S(2)}, u32[]{:S(2)}) async-start(bf16[16,48,1152]{2,1,0:T(8,128)(2,1)} %param.10), calls=%async_computation | async-start | bytes 3538944 | tf_op jit(solution)/shard_map/all_to_all | solution.py:288
  8.6 6.4 %copy.16.w_qkv = bf16[1152,1728]{1,0:T(8,128)(2,1)} copy(bf16[1152,1728]{0,1:T(8,128)(2,1)} %param.17) | data formatting | bytes 7962624 | tf_op args[7]
  15.1 31.0 %temporal.1 = (bf16[16,48,1152]{2,1,0:T(8,128)(2,1)}, f32[3,1152]{1,0:T(4,128)}) custom-call(bf16[3,16,48,576]{3,2,1,0:T(8,128)(2,1)} %qkv.1, bf16[16,48,1152]{2,1,0:T(8,128)(2,1)} %og.1, bf16[16,48,1152]{2,1,0:T(8,128)(2,1)} %u.1, f32[5,1152]{1,0:T(8,128)} %mod.7, f32[4,576]{1,0:T(4,128)} %tile.10.gains, bf16[576,1152]{1,0:T(8,128)(2,1)} %w_out.3, ...), custom_call_target="tpu_custom_call" | custom-call | flops 10192158720 | bytes 12582912 | tf_op jit(solution)/shard_map/temporal/pallas_call | solution.py:172
  46.1 3.0 %all-to-all-done = bf16[16,48,1152]{2,1,0:T(8,128)(2,1)S(1)} async-done(((bf16[16,48,1152]{2,1,0:T(8,128)(2,1)}), bf16[16,48,1152]{2,1,0:T(8,128)(2,1)S(1)}, u32[]{:S(2)}, u32[]{:S(2)}) %all-to-all-start) | async-done | bytes 1769504 | tf_op jit(solution)/shard_map/all_to_all | solution.py:288
  49.2 1.2 copy-done.1
  50.4 3.6 %all-to-all-start.1 = ((bf16[16,48,1152]{2,1,0:T(8,128)(2,1)}), bf16[16,48,1152]{2,1,0:T(8,128)(2,1)S(1)}, u32[]{:S(2)}, u32[]{:S(2)}) async-start(bf16[16,48,1152]{2,1,0:T(8,128)(2,1)} %get-tuple-element.11), calls=%async_computation.1 | async-start | bytes 3538944 | tf_op jit(solution)/shard_map/all_to_all | solution.py:288
  54.0 6.5 %copy.17.w_qkv = bf16[1152,1728]{1,0:T(8,128)(2,1)} copy(bf16[1152,1728]{0,1:T(8,128)(2,1)} %param.15) | data formatting | bytes 7962624 | tf_op args[5]
  60.5 8.0 %project.1 = (bf16[2,384,576]{2,1,0:T(8,128)(2,1)}, bf16[2,384,576]{2,1,0:T(8,128)(2,1)}, bf16[2,384,576]{2,1,0:T(8,128)(2,1)}) custom-call(bf16[8,2,48,1152]{3,2,1,0:T(8,128)(2,1)} %bitcast.5, f32[5,1152]{1,0:T(8,128)} %mod.7, bf16[1152,1728]{1,0:T(8,128)(2,1)} %copy.17.w_qkv), custom_call_target="tpu_custom_call" | custom-call | flops 3057647616 | bytes 8388608 | tf_op jit(solution)/shard_map/project/pallas_call | solution.py:207
  68.4 27.0 %all-to-all-done.1 = bf16[16,48,1152]{2,1,0:T(8,128)(2,1)S(1)} async-done(((bf16[16,48,1152]{2,1,0:T(8,128)(2,1)}), bf16[16,48,1152]{2,1,0:T(8,128)(2,1)S(1)}, u32[]{:S(2)}, u32[]{:S(2)}) %all-to-all-start.1) | async-done | bytes 1769504 | tf_op jit(solution)/shard_map/all_to_all | solution.py:288
  95.4 1.2 copy-done.2
  96.6 14.6 %spatial.3 = (bf16[8,48,1152]{2,1,0:T(8,128)(2,1)}, f32[3,1152]{1,0:T(4,128)}) custom-call(bf16[8,2,48,1152]{3,2,1,0:T(8,128)(2,1)} %bitcast.6, bf16[8,2,48,1152]{3,2,1,0:T(8,128)(2,1)} %bitcast.8, bf16[2,384,576]{2,1,0:T(8,128)(2,1)} %get-tuple-element.12.q, bf16[2,384,576]{2,1,0:T(8,128)(2,1)} %get-tuple-element.13.k, ...), custom_call_target="tpu_custom_call" | custom-call | flops 7134511104 | bytes 8388608 | tf_op jit(solution)/shard_map/spatial/pallas_call | solution.py:262
  111.2 14.9 %spatial.2 = (bf16[8,48,1152]{2,1,0:T(8,128)(2,1)}, f32[3,1152]{1,0:T(4,128)}) custom-call(bf16[8,2,48,1152]{3,2,1,0:T(8,128)(2,1)} %bitcast.7, bf16[8,2,48,1152]{3,2,1,0:T(8,128)(2,1)} %bitcast.9, bf16[2,384,576]{2,1,0:T(8,128)(2,1)} %get-tuple-element.12.q, bf16[2,384,576]{2,1,0:T(8,128)(2,1)} %get-tuple-element.13.k, ...), custom_call_target="tpu_custom_call" | custom-call | flops 7134511104 | bytes 8388608 | tf_op jit(solution)/shard_map/spatial/pallas_call | solution.py:262
  126.2 1.3 pad_maximum_fusion
  127.5 1.3 copy.20
  128.9 3.8 %all-to-all-start.2 = ((bf16[16,48,1152]{2,1,0:T(8,128)(2,1)}), bf16[16,48,1152]{2,1,0:T(8,128)(2,1)S(1)}, u32[]{:S(2)}, u32[]{:S(2)}) async-start(bf16[16,48,1152]{2,1,0:T(8,128)(2,1)} %bitcast.4), calls=%async_computation.2 | async-start | bytes 3538944 | tf_op jit(solution)/shard_map/all_to_all | solution.py:288
  132.6 0.7 add.16
  133.4 0.7 pad_maximum_fusion.1
  134.1 3.0 %collective-permute-start = (f32[6,1152]{1,0:T(8,128)S(1)}, f32[6,1152]{1,0:T(8,128)S(1)}, u32[]{:S(2)}, u32[]{:S(2)}) collective-permute-start(f32[6,1152]{1,0:T(8,128)S(1)} %pad_maximum_fusion.1), channel_id=1, source_target_pairs={{0,4},{1,5},{2,6},{3,7},{4,0},{5,1},{6,2},{7,3},{8,12},{9,13},{10,... | collective-permute-start | bytes 82952 | tf_op jit(solution)/shard_map/ppermute | solution.py:282
  137.1 38.5 %collective-permute-done = f32[6,1152]{1,0:T(8,128)S(1)} collective-permute-done((f32[6,1152]{1,0:T(8,128)S(1)}, f32[6,1152]{1,0:T(8,128)S(1)}, u32[]{:S(2)}, u32[]{:S(2)}) %collective-permute-start) | collective-permute-done | bytes 27680 | tf_op jit(solution)/shard_map/ppermute | solution.py:282
  175.6 0.7 fusion
  176.4 3.9 %collective-permute-done.1 = f32[6,1152]{1,0:T(8,128)S(1)} collective-permute-done((f32[6,1152]{1,0:T(8,128)S(1)}, f32[6,1152]{1,0:T(8,128)S(1)}, u32[]{:S(2)}, u32[]{:S(2)}) %collective-permute-start.1) | collective-permute-done | bytes 27680 | tf_op jit(solution)/shard_map/ppermute | solution.py:282
  180.4 1.5 collective-permute-start.2
  181.8 2.5 %collective-permute-done.2 = f32[6,1152]{1,0:T(8,128)S(1)} collective-permute-done((f32[6,1152]{1,0:T(8,128)S(1)}, f32[6,1152]{1,0:T(8,128)S(1)}, u32[]{:S(2)}, u32[]{:S(2)}) %collective-permute-start.2) | collective-permute-done | bytes 27680 | tf_op jit(solution)/shard_map/ppermute | solution.py:282
  185.0 1.6 add_convert_fusion
  (14 shorter events, 1.4 us)
Async XLA Ops:
  0.6 7.3 %copy-start.4 = (f32[4,72]{1,0:T(4,128)S(1)}, f32[4,72]{1,0:T(4,128)}, u32[]{:S(2)}) copy-start(f32[4,72]{1,0:T(4,128)} %param.19) | copy-start | bytes 3460
  0.6 48.5 %all-to-all-start = ((bf16[16,48,1152]{2,1,0:T(8,128)(2,1)}), bf16[16,48,1152]{2,1,0:T(8,128)(2,1)S(1)}, u32[]{:S(2)}, u32[]{:S(2)}) async-start(bf16[16,48,1152]{2,1,0:T(8,128)(2,1)} %param.10), calls=%async_computation | async-start | bytes 3538944 | tf_op jit(solution)/shard_map/all_to_all | solution.py:288
  49.1 1.2 copy-start.1
  50.4 45.0 %all-to-all-start.1 = ((bf16[16,48,1152]{2,1,0:T(8,128)(2,1)}), bf16[16,48,1152]{2,1,0:T(8,128)(2,1)S(1)}, u32[]{:S(2)}, u32[]{:S(2)}) async-start(bf16[16,48,1152]{2,1,0:T(8,128)(2,1)} %get-tuple-element.11), calls=%async_computation.1 | async-start | bytes 3538944 | tf_op jit(solution)/shard_map/all_to_all | solution.py:288
  95.4 1.2 copy-start.2
  111.2 14.9 %copy-start.3 = (bf16[8,48,1152]{2,1,0:T(8,128)(2,1)S(1)}, bf16[8,48,1152]{2,1,0:T(8,128)(2,1)}, u32[]{:S(2)}) copy-start(bf16[8,48,1152]{2,1,0:T(8,128)(2,1)} %get-tuple-element.16) | copy-start | bytes 2654212
  128.9 56.1 %copy-start = (bf16[16,48,1152]{2,1,0:T(8,128)(2,1)S(1)}, bf16[16,48,1152]{2,1,0:T(8,128)(2,1)}, u32[]{:S(2)}) copy-start(bf16[16,48,1152]{2,1,0:T(8,128)(2,1)} %get-tuple-element.11) | copy-start | bytes 5308420
  128.9 56.1 %all-to-all-start.2 = ((bf16[16,48,1152]{2,1,0:T(8,128)(2,1)}), bf16[16,48,1152]{2,1,0:T(8,128)(2,1)S(1)}, u32[]{:S(2)}, u32[]{:S(2)}) async-start(bf16[16,48,1152]{2,1,0:T(8,128)(2,1)} %bitcast.4), calls=%async_computation.2 | async-start | bytes 3538944 | tf_op jit(solution)/shard_map/all_to_all | solution.py:288
  134.1 41.5 %collective-permute-start = (f32[6,1152]{1,0:T(8,128)S(1)}, f32[6,1152]{1,0:T(8,128)S(1)}, u32[]{:S(2)}, u32[]{:S(2)}) collective-permute-start(f32[6,1152]{1,0:T(8,128)S(1)} %pad_maximum_fusion.1), channel_id=1, source_target_pairs={{0,4},{1,5},{2,6},{3,7},{4,0},{5,1},{6,2},{7,3},{8,12},{9,13},{10,... | collective-permute-start | bytes 82952 | tf_op jit(solution)/shard_map/ppermute | solution.py:282
  176.3 4.0 %collective-permute-start.1 = (f32[6,1152]{1,0:T(8,128)S(1)}, f32[6,1152]{1,0:T(8,128)S(1)}, u32[]{:S(2)}, u32[]{:S(2)}) collective-permute-start(f32[6,1152]{1,0:T(8,128)S(1)} %fusion), channel_id=1, source_target_pairs={{0,2},{1,3},{2,0},{3,1},{4,6},{5,7},{6,4},{7,5},{8,10},{9,11},{10,... | collective-permute-start | bytes 82952 | tf_op jit(solution)/shard_map/ppermute | solution.py:282
  180.4 4.0 %collective-permute-start.2 = (f32[6,1152]{1,0:T(8,128)S(1)}, f32[6,1152]{1,0:T(8,128)S(1)}, u32[]{:S(2)}, u32[]{:S(2)}) collective-permute-start(f32[6,1152]{1,0:T(8,128)S(1)} %add.18), channel_id=1, source_target_pairs={{0,1},{1,0},{2,3},{3,2},{4,5},{5,4},{6,7},{7,6},{8,9},{9,8},{10,11... | collective-permute-start | bytes 82952 | tf_op jit(solution)/shard_map/ppermute | solution.py:282
